TPU v7x, 32 devices: a whole 2x2x4 slice. The times are simulated.
32 devices in a mesh: dp: 8 (over z, x), var: 4 (over y, core).
Axes of the slice: x: 2, y: 2, z: 4, core: 2. Of those that a mesh axis runs over, the one named last changes fastest.
Arguments:
- pixels: bfloat16 [8, 24, 4, 256], P('dp', 'var'), may hold values from -6 to 6
- var_ids: int32 [8, 24], P('dp', 'var'), may hold values from 0 to 90, as said below
- counts: int32 [8], P('dp'), may hold values from 3 to 24, as said below
- patch_weight: bfloat16 [91, 4, 1024], replicated, may hold values from -3 to 3
- var_embed: bfloat16 [91, 1024], replicated, may hold values from -5 to 5
- norm_gain: float32 [1024], replicated, may hold values from 0.1 to 1.9
- norm_bias: float32 [1024], replicated, may hold values from -3 to 3
- key_weight: bfloat16 [1024, 1024], P('dp'), may hold values from -0.1875 to 0.1875
- value_weight: bfloat16 [1024, 1024], P('dp'), may hold values from -0.1875 to 0.1875
- query: float32 [16, 64], replicated, may hold values from -200 to 200
- out_weight: bfloat16 [1024, 1024], replicated, may hold values from -0.1875 to 0.1875
Outputs:
- aggregated: bfloat16 [8, 256, 1024], P('dp', 'var')
Inputs may be any that keep to these rules, and one draw needn't show every extreme that they name: `var_ids`: in each sample the ids of slots below its count are distinct; slots at or past the count are padding with arbitrary ids. `counts`: some sample has exactly min(91, 24) live slots and some has exactly 3.
All inputs are finite; a program needn't handle non-finite values.
Results may differ from a plain program's by a relative error of at most 0.018.
Values may be sent and summed in bfloat16 or wider, within the bound.
A program may use at most 64 MiB of HBM per device.

v0:
```python
import functools
import math

import jax
import jax.numpy as jnp
from jax import lax
from jax.experimental import pallas as pl
from jax.experimental.pallas import tpu as pltpu
from jax.sharding import PartitionSpec as P

F32 = jnp.float32
BF16 = jnp.bfloat16
EXACT = lax.Precision.HIGHEST


def rounded_up(value, unit):
    return -(-value // unit) * unit


def kernel(
    dims,
    ids_ref,
    counts_ref,
    pixels_ref,
    table_hbm,
    embed_hbm,
    gain_ref,
    bias_ref,
    key_hbm,
    value_hbm,
    query_ref,
    out_hbm,
    result_ref,
    table,
    embed,
    key_block,
    wout,
    value_all,
    fold_all,
    rows_f32,
    rows_all,
    coeff_all,
    basis,
    mix_send,
    mix_recv,
    local_sem,
    value_ss,
    value_rs,
    fold_ss,
    fold_rs,
    rows_ss,
    rows_rs,
    coeff_ss,
    coeff_rs,
    mix_ss,
    mix_rs,
):
    n, nv, groups, slots, taps, patches, width, heads, head_size = dims
    padded = rows_f32.shape[1]
    depth = key_block.shape[0]
    columns = key_block.shape[1]
    local_heads = heads // groups
    half = patches * groups // nv
    owned = patches // nv
    basis_rows = nv * (taps + 2) * padded

    b = lax.axis_index("dp")
    v = lax.axis_index("var")
    r, g = v // groups, v % groups
    pair = n % 2 == 0
    lo_size = 2 if pair else 1
    hi_size = n // lo_size
    hi, lo = b // lo_size, b % lo_size

    def remote(src, dst, ss, rs, **where):
        return pltpu.make_async_remote_copy(
            src_ref=src,
            dst_ref=dst,
            send_sem=ss,
            recv_sem=rs,
            device_id=where,
            device_id_type=pl.DeviceIdType.MESH,
        )

    barrier = pltpu.get_barrier_semaphore()
    for off in range(1, n):
        pl.semaphore_signal(
            barrier, inc=1, device_id={"dp": (b + off) % n}, device_id_type=pl.DeviceIdType.MESH
        )
    for off in range(1, nv):
        pl.semaphore_signal(
            barrier, inc=1, device_id={"var": (v + off) % nv}, device_id_type=pl.DeviceIdType.MESH
        )

    mine = pl.ds(pl.multiple_of(g * columns, columns), columns)
    get_key = pltpu.make_async_copy(key_hbm.at[:, mine], key_block, local_sem.at[0])
    get_value = pltpu.make_async_copy(value_hbm.at[:, mine], value_all.at[b], local_sem.at[1])
    get_table = pltpu.make_async_copy(table_hbm, table, local_sem.at[2])
    get_embed = pltpu.make_async_copy(embed_hbm, embed, local_sem.at[3])
    get_out = pltpu.make_async_copy(out_hbm, wout, local_sem.at[4])
    get_value.start()
    get_key.start()
    get_table.start()
    get_embed.start()
    get_out.start()

    fold_rows = fold_all.shape[1]
    pick = (
        lax.broadcasted_iota(jnp.int32, (fold_rows, heads), 1)
        == lax.broadcasted_iota(jnp.int32, (fold_rows, heads), 0) + g * local_heads
    ).astype(F32)
    own_query = jnp.dot(pick, query_ref[...], precision=EXACT, preferred_element_type=F32)
    spread_out = (
        lax.broadcasted_iota(jnp.int32, (head_size, columns), 1) % head_size
        == lax.broadcasted_iota(jnp.int32, (head_size, columns), 0)
    ).astype(F32)
    tiled = jnp.dot(own_query, spread_out, precision=EXACT, preferred_element_type=F32)
    own_head = (
        lax.broadcasted_iota(jnp.int32, (fold_rows, columns), 1) // head_size
        == lax.broadcasted_iota(jnp.int32, (fold_rows, columns), 0)
    )
    diagonal = jnp.where(own_head, tiled, 0.0) * (1.0 / math.sqrt(head_size))

    get_value.wait()
    pl.semaphore_wait(barrier, n + nv - 2)

    value_sends = []

    def send_value(owner, sem, **where):
        copy = remote(
            value_all.at[owner], value_all.at[owner], value_ss.at[sem], value_rs.at[sem], **where
        )
        copy.start()
        value_sends.append(copy)

    def value_from(owner, sem):
        return remote(
            value_all.at[owner], value_all.at[owner], value_ss.at[sem], value_rs.at[sem], dp=b
        )

    mate = hi * lo_size + (lo_size - 1 - lo)
    if pair:
        send_value(b, hi_size, dp=mate)
    for off in range(1, hi_size):
        send_value(b, off, dp=((hi + off) % hi_size) * lo_size + lo)

    get_key.wait()
    fold_all[b] = lax.dot_general(
        diagonal,
        key_block[...].astype(F32),
        (((1,), (1,)), ((), ())),
        precision=EXACT,
        preferred_element_type=F32,
    )

    rows_f32[...] = jnp.zeros_like(rows_f32)
    get_table.wait()
    get_embed.wait()
    slot_of = lax.broadcasted_iota(jnp.int32, (padded, embed.shape[0]), 0)
    wanted = jnp.full((padded, embed.shape[0]), -1, jnp.int32)
    for s in range(slots):
        rows = table[ids_ref[0, s]].astype(F32)
        for k in range(taps):
            rows_f32[k, s : s + 1, :] = rows[k : k + 1, :]
        wanted = jnp.where(slot_of == s, ids_ref[0, s], wanted)
    hot = (wanted == lax.broadcasted_iota(jnp.int32, wanted.shape, 1)).astype(BF16)
    rows_f32[taps] = jnp.dot(hot, embed[...], preferred_element_type=F32)
    rows_all[v] = rows_f32[...].astype(BF16)

    fold_sends = []
    for off in range(1, n):
        copy = remote(
            fold_all.at[b], fold_all.at[b], fold_ss.at[off], fold_rs.at[off], dp=(b + off) % n
        )
        copy.start()
        fold_sends.append(copy)

    centred = []
    for k in range(taps + 1):
        row = rows_f32[k]
        centred.append(row - jnp.mean(row, axis=-1, keepdims=True))

    rows_sends = []
    for off in range(1, nv):
        copy = remote(
            rows_all.at[v], rows_all.at[v], rows_ss.at[off], rows_rs.at[off], var=(v + off) % nv
        )
        copy.start()
        rows_sends.append(copy)

    pix = pixels_ref[0].astype(F32)
    fill = jnp.zeros((padded - slots, patches), F32)
    field = []
    for k in range(taps):
        own = [pix[s, k : k + 1, :] for s in range(slots)]
        field.append(jnp.concatenate(own + ([fill] if padded > slots else []), axis=0))
    field.append(jnp.ones((padded, patches), F32))
    variance = jnp.zeros((padded, patches), F32)
    for k in range(taps + 1):
        for m in range(k, taps + 1):
            gram = jnp.mean(centred[k] * centred[m], axis=-1, keepdims=True)
            variance += (1.0 if m == k else 2.0) * gram * (field[k] * field[m])
    scale = lax.rsqrt(jnp.maximum(variance, 0.0) + 1e-05)
    for k in range(taps + 1):
        coeff_all[v, k] = field[k] * scale

    def forward(off):
        owner = ((hi + hi_size - off) % hi_size) * lo_size + lo
        value_from(owner, off).wait_recv()
        if pair:
            send_value(owner, hi_size + off, dp=mate)

    if hi_size > 1:
        forward(1)
    coeff_sends = []
    for off in range(1, nv):
        copy = remote(
            coeff_all.at[v], coeff_all.at[v], coeff_ss.at[off], coeff_rs.at[off], var=(v + off) % nv
        )
        copy.start()
        coeff_sends.append(copy)
    for off in range(2, hi_size):
        forward(off)

    gain = gain_ref[...]
    for off in range(nv):
        src = (v + nv - off) % nv
        if off:
            remote(
                rows_all.at[src], rows_all.at[src], rows_ss.at[off], rows_rs.at[off], var=v
            ).wait_recv()
        for k in range(taps + 1):
            row = rows_all[src, k].astype(F32)
            basis[src, k] = (row - jnp.mean(row, axis=-1, keepdims=True)) * gain
        basis[src, taps + 1] = jnp.broadcast_to(bias_ref[...], (padded, width))

    for off in range(1, n):
        src = (b + n - off) % n
        remote(
            fold_all.at[src], fold_all.at[src], fold_ss.at[off], fold_rs.at[off], dp=b
        ).wait_recv()
    flat = basis[...].reshape(basis_rows, width)
    folded = jnp.concatenate([fold_all[i] for i in range(n)], axis=1)
    score_of = lax.dot_general(
        flat, folded, (((1,), (1,)), ((), ())), precision=EXACT, preferred_element_type=F32
    ).reshape(nv, taps + 2, padded, fold_rows)

    for off in range(1, nv):
        src = (v + nv - off) % nv
        remote(
            coeff_all.at[src], coeff_all.at[src], coeff_ss.at[off], coeff_rs.at[off], var=v
        ).wait_recv()
    window = pl.ds(pl.multiple_of(r * half, half), half)
    coeff = [coeff_all[:, k, :, window] for k in range(taps + 1)]
    place = lax.broadcasted_iota(jnp.int32, (nv, padded, half), 1)
    slot = lax.broadcasted_iota(jnp.int32, (nv, padded, half), 0) * slots + place
    live = (place < slots) & (slot < counts_ref[0])
    weights = []
    for h in range(local_heads):
        score = jnp.broadcast_to(score_of[:, taps + 1, :, h : h + 1], (nv, padded, half))
        for k in range(taps + 1):
            score = score + coeff[k] * score_of[:, k, :, h : h + 1]
        score = jnp.where(live, score, -1e30)
        peak = jnp.max(jnp.max(score, axis=0, keepdims=True), axis=1, keepdims=True)
        expo = jnp.exp(score - peak)
        total = jnp.sum(jnp.sum(expo, axis=0, keepdims=True), axis=1, keepdims=True)
        prob = expo / total
        parts = [prob * coeff[k] for k in range(taps + 1)] + [prob]
        weights.append(jnp.stack(parts, axis=1).reshape(basis_rows, half).astype(BF16))

    if pair:
        for off in range(hi_size):
            owner = ((hi + hi_size - off) % hi_size) * lo_size + (lo_size - 1 - lo)
            value_from(owner, hi_size + off).wait_recv()
    projected = jnp.dot(
        flat.astype(BF16),
        value_all[...].reshape(width, columns),
        preferred_element_type=F32,
    ).astype(BF16)
    mixed = jnp.concatenate(
        [
            lax.dot_general(
                weights[h],
                projected[:, h * head_size : (h + 1) * head_size],
                (((0,), (0,)), ((), ())),
                preferred_element_type=F32,
            )
            for h in range(local_heads)
        ],
        axis=1,
    ).astype(BF16)
    mix_send[...] = mixed.reshape(groups, owned, columns)

    mix_sends = []
    for off in range(1, groups):
        to = (g + off) % groups
        copy = remote(
            mix_send.at[to], mix_recv.at[g], mix_ss.at[off], mix_rs.at[off], var=r * groups + to
        )
        copy.start()
        mix_sends.append(copy)

    get_out.wait()
    total = jnp.dot(mix_send[g], wout[mine, :], preferred_element_type=F32)
    for off in range(1, groups):
        src = (g + groups - off) % groups
        remote(
            mix_send.at[src], mix_recv.at[src], mix_ss.at[off], mix_rs.at[off], var=v
        ).wait_recv()
        there = pl.ds(pl.multiple_of(src * columns, columns), columns)
        total += jnp.dot(mix_recv[src], wout[there, :], preferred_element_type=F32)
    result_ref[0] = total.astype(result_ref.dtype)

    for copy in value_sends + fold_sends + rows_sends + coeff_sends + mix_sends:
        copy.wait_send()


def on_device(
    n,
    nv,
    pixels,
    var_ids,
    counts,
    patch_weight,
    var_embed,
    norm_gain,
    norm_bias,
    key_weight,
    value_weight,
    query,
    out_weight,
):
    slots, taps, patches = pixels.shape[1:]
    width = out_weight.shape[0]
    heads, head_size = query.shape
    groups = min(nv, width // 128)
    columns = width // groups
    depth = value_weight.shape[0]
    padded = rounded_up(slots, 8)
    owned = patches // nv
    fold_rows = rounded_up(heads // groups, 8)
    vmem = pl.BlockSpec(memory_space=pltpu.VMEM)
    smem = pl.BlockSpec(memory_space=pltpu.SMEM)
    hbm = pl.BlockSpec(memory_space=pl.ANY)
    dims = (n, nv, groups, slots, taps, patches, width, heads, head_size)
    dma = pltpu.SemaphoreType.DMA
    return pl.pallas_call(
        functools.partial(kernel, dims),
        out_shape=jax.ShapeDtypeStruct((1, owned, width), BF16),
        in_specs=[smem, smem, vmem, hbm, hbm, vmem, vmem, hbm, hbm, vmem, hbm],
        out_specs=vmem,
        scratch_shapes=[
            pltpu.VMEM(patch_weight.shape, BF16),
            pltpu.VMEM(var_embed.shape, BF16),
            pltpu.VMEM((depth, columns), BF16),
            pltpu.VMEM((width, width), BF16),
            pltpu.VMEM((n, depth, columns), BF16),
            pltpu.VMEM((n, fold_rows, depth), F32),
            pltpu.VMEM((taps + 1, padded, width), F32),
            pltpu.VMEM((nv, taps + 1, padded, width), BF16),
            pltpu.VMEM((nv, taps + 1, padded, patches), F32),
            pltpu.VMEM((nv, taps + 2, padded, width), F32),
            pltpu.VMEM((groups, owned, columns), BF16),
            pltpu.VMEM((groups, owned, columns), BF16),
            dma((5,)),
            dma((n,)),
            dma((n,)),
            dma((n,)),
            dma((n,)),
            dma((nv,)),
            dma((nv,)),
            dma((nv,)),
            dma((nv,)),
            dma((groups,)),
            dma((groups,)),
        ],
        compiler_params=pltpu.CompilerParams(collective_id=0, has_side_effects=True),
    )(
        var_ids,
        counts,
        pixels,
        patch_weight,
        var_embed,
        norm_gain.reshape(1, width),
        norm_bias.reshape(1, width),
        key_weight,
        value_weight,
        query,
        out_weight,
    )


def solution(mesh):
    placed = (
        P("dp", "var", None, None),
        P("dp", "var"),
        P("dp"),
        P(),
        P(),
        P(),
        P(),
        P("dp", None),
        P("dp", None),
        P(),
        P(),
    )
    return jax.shard_map(
        functools.partial(on_device, mesh.shape["dp"], mesh.shape["var"]),
        mesh=mesh,
        in_specs=placed,
        out_specs=P("dp", "var", None),
        check_vma=False,
    )
```

profile of v0, /device:TPU:0, one launch (start us, length us, event | category | flops | bytes accessed | tf_op | source)
XLA Modules:
  0.0 24.6 jit_solution(9116692624541389698)
XLA Ops:
  0.7 22.4 %shard_map.109 = bf16[1,64,1024]{2,1,0:T(8,128)(2,1)} custom-call(s32[1,6]{1,0:T(1,128)} %ids_ref.1, s32[1]{0:T(128)S(6)} %copy.13.counts_ref, bf16[1,6,4,256]{3,2,1,0:T(4,128)(2,1)} %pixels_ref.1, bf16[91,4,1024]{2,1,0:T(4,128)(2,1)} %table_hbm.1, bf16[91,1024]{1,0:T(8,128)(2,1)} %embed_hbm.1, f32[1,1024]{1,0:T(1,128)} %bitcast.2, f32[1,1024]{1,0:T(1,128)} %bitcast.3, ...), custom_call_target="tpu_custom_call" | custom-call | tf_op jit(solution)/shard_map/pallas_call | solution.py:347
  23.1 1.6 %copy.14 = bf16[1,64,1024]{2,1,0:T(8,128)(2,1)} copy(bf16[1,64,1024]{2,1,0:T(8,128)(2,1)} %shard_map.109) | data formatting | bytes 262144
where the time goes:
time: 24.8 us; the launch traced here: 24.6 us
  Pallas kernels  22.4 us (90%)
  local copies, waits for them, and re-layouts  1.57 us (6%)
  between operations  0.66 us (3%)
    pallas_call x1, Pallas kernels, on_device(): pl.pallas_call(functools.partial(kernel, dims), out_shape=jax.ShapeDtypeS...  22.4 us
    unnamed x1, local copies, waits for them, and re-layouts  1.57 us

commit v1 on v0

--- a/solution.py
+++ b/solution.py
@@ -19,18 +19,24 @@
 
 def kernel(
     dims,
+    ids_hbm,
+    counts_hbm,
+    pixels_hbm,
+    table_hbm,
+    embed_hbm,
+    gain_hbm,
+    bias_hbm,
+    key_hbm,
+    value_hbm,
+    query_hbm,
+    out_hbm,
+    result_ref,
     ids_ref,
     counts_ref,
     pixels_ref,
-    table_hbm,
-    embed_hbm,
     gain_ref,
     bias_ref,
-    key_hbm,
-    value_hbm,
     query_ref,
-    out_hbm,
-    result_ref,
     table,
     embed,
     key_block,
@@ -93,18 +99,31 @@
         )
 
     mine = pl.ds(pl.multiple_of(g * columns, columns), columns)
+    get_query = pltpu.make_async_copy(query_hbm, query_ref, local_sem.at[5])
+    get_ids = pltpu.make_async_copy(ids_hbm, ids_ref, local_sem.at[6])
+    get_pixels = pltpu.make_async_copy(pixels_hbm, pixels_ref, local_sem.at[7])
+    get_gain = pltpu.make_async_copy(gain_hbm, gain_ref, local_sem.at[8])
+    get_bias = pltpu.make_async_copy(bias_hbm, bias_ref, local_sem.at[9])
+    get_counts = pltpu.make_async_copy(counts_hbm, counts_ref, local_sem.at[10])
     get_key = pltpu.make_async_copy(key_hbm.at[:, mine], key_block, local_sem.at[0])
     get_value = pltpu.make_async_copy(value_hbm.at[:, mine], value_all.at[b], local_sem.at[1])
     get_table = pltpu.make_async_copy(table_hbm, table, local_sem.at[2])
     get_embed = pltpu.make_async_copy(embed_hbm, embed, local_sem.at[3])
     get_out = pltpu.make_async_copy(out_hbm, wout, local_sem.at[4])
     get_value.start()
+    get_query.start()
     get_key.start()
+    get_ids.start()
+    get_pixels.start()
     get_table.start()
     get_embed.start()
+    get_gain.start()
+    get_bias.start()
+    get_counts.start()
     get_out.start()
 
     fold_rows = fold_all.shape[1]
+    get_query.wait()
     pick = (
         lax.broadcasted_iota(jnp.int32, (fold_rows, heads), 1)
         == lax.broadcasted_iota(jnp.int32, (fold_rows, heads), 0) + g * local_heads
@@ -121,29 +140,6 @@
     )
     diagonal = jnp.where(own_head, tiled, 0.0) * (1.0 / math.sqrt(head_size))
 
-    get_value.wait()
-    pl.semaphore_wait(barrier, n + nv - 2)
-
-    value_sends = []
-
-    def send_value(owner, sem, **where):
-        copy = remote(
-            value_all.at[owner], value_all.at[owner], value_ss.at[sem], value_rs.at[sem], **where
-        )
-        copy.start()
-        value_sends.append(copy)
-
-    def value_from(owner, sem):
-        return remote(
-            value_all.at[owner], value_all.at[owner], value_ss.at[sem], value_rs.at[sem], dp=b
-        )
-
-    mate = hi * lo_size + (lo_size - 1 - lo)
-    if pair:
-        send_value(b, hi_size, dp=mate)
-    for off in range(1, hi_size):
-        send_value(b, off, dp=((hi + off) % hi_size) * lo_size + lo)
-
     get_key.wait()
     fold_all[b] = lax.dot_general(
         diagonal,
@@ -152,8 +148,40 @@
         precision=EXACT,
         preferred_element_type=F32,
     )
+    get_value.wait()
+    pl.semaphore_wait(barrier, n + nv - 2)
+
+    fold_sends = []
+    for off in range(1, n):
+        copy = remote(
+            fold_all.at[b], fold_all.at[b], fold_ss.at[off], fold_rs.at[off], dp=(b + off) % n
+        )
+        copy.start()
+        fold_sends.append(copy)
+
+    value_sends = []
+
+    def send_value(owner, sem, **where):
+        copy = remote(
+            value_all.at[owner], value_all.at[owner], value_ss.at[sem], value_rs.at[sem], **where
+        )
+        copy.start()
+        value_sends.append(copy)
+
+    def value_from(owner, sem):
+        return remote(
+            value_all.at[owner], value_all.at[owner], value_ss.at[sem], value_rs.at[sem], dp=b
+        )
+
+    mate = hi * lo_size + (lo_size - 1 - lo)
+    if pair:
+        send_value(b, hi_size, dp=mate)
+    for off in range(1, hi_size):
+        send_value(b, off, dp=((hi + off) % hi_size) * lo_size + lo)
+
 
     rows_f32[...] = jnp.zeros_like(rows_f32)
+    get_ids.wait()
     get_table.wait()
     get_embed.wait()
     slot_of = lax.broadcasted_iota(jnp.int32, (padded, embed.shape[0]), 0)
@@ -167,13 +195,6 @@
     rows_f32[taps] = jnp.dot(hot, embed[...], preferred_element_type=F32)
     rows_all[v] = rows_f32[...].astype(BF16)
 
-    fold_sends = []
-    for off in range(1, n):
-        copy = remote(
-            fold_all.at[b], fold_all.at[b], fold_ss.at[off], fold_rs.at[off], dp=(b + off) % n
-        )
-        copy.start()
-        fold_sends.append(copy)
 
     centred = []
     for k in range(taps + 1):
@@ -188,6 +209,7 @@
         copy.start()
         rows_sends.append(copy)
 
+    get_pixels.wait()
     pix = pixels_ref[0].astype(F32)
     fill = jnp.zeros((padded - slots, patches), F32)
     field = []
@@ -222,6 +244,8 @@
     for off in range(2, hi_size):
         forward(off)
 
+    get_gain.wait()
+    get_bias.wait()
     gain = gain_ref[...]
     for off in range(nv):
         src = (v + nv - off) % nv
@@ -250,6 +274,7 @@
         remote(
             coeff_all.at[src], coeff_all.at[src], coeff_ss.at[off], coeff_rs.at[off], var=v
         ).wait_recv()
+    get_counts.wait()
     window = pl.ds(pl.multiple_of(r * half, half), half)
     coeff = [coeff_all[:, k, :, window] for k in range(taps + 1)]
     place = lax.broadcasted_iota(jnp.int32, (nv, padded, half), 1)
@@ -340,16 +365,21 @@
     owned = patches // nv
     fold_rows = rounded_up(heads // groups, 8)
     vmem = pl.BlockSpec(memory_space=pltpu.VMEM)
-    smem = pl.BlockSpec(memory_space=pltpu.SMEM)
     hbm = pl.BlockSpec(memory_space=pl.ANY)
     dims = (n, nv, groups, slots, taps, patches, width, heads, head_size)
     dma = pltpu.SemaphoreType.DMA
     return pl.pallas_call(
         functools.partial(kernel, dims),
-        out_shape=jax.ShapeDtypeStruct((1, owned, width), BF16),
-        in_specs=[smem, smem, vmem, hbm, hbm, vmem, vmem, hbm, hbm, vmem, hbm],
+        out_shape=pltpu.VMEM((1, owned, width), BF16),
+        in_specs=[pl.BlockSpec(memory_space=pltpu.HBM)] * 11,
         out_specs=vmem,
         scratch_shapes=[
+            pltpu.SMEM(var_ids.shape, jnp.int32),
+            pltpu.SMEM(counts.shape, jnp.int32),
+            pltpu.VMEM(pixels.shape, BF16),
+            pltpu.VMEM((1, width), F32),
+            pltpu.VMEM((1, width), F32),
+            pltpu.VMEM(query.shape, F32),
             pltpu.VMEM(patch_weight.shape, BF16),
             pltpu.VMEM(var_embed.shape, BF16),
             pltpu.VMEM((depth, columns), BF16),
@@ -362,7 +392,7 @@
             pltpu.VMEM((nv, taps + 2, padded, width), F32),
             pltpu.VMEM((groups, owned, columns), BF16),
             pltpu.VMEM((groups, owned, columns), BF16),
-            dma((5,)),
+            dma((11,)),
             dma((n,)),
             dma((n,)),
             dma((n,)),

time: 24.8 us -> 23.1 us (0.931)
  local copies, waits for them, and re-layouts: 1.57 us -> 0.66 us
  Pallas kernels: 22.4 us -> 21.6 us
    unnamed x1, local copies, waits for them, and re-layouts: 1.57 us -> 0.66 us
    pallas_call x1, Pallas kernels: 22.4 us -> 21.6 us  [on_device(): pl.pallas_call(functools.partial(kernel, dims), out_shape=pltpu.VMEM((1,...]
where the time goes in v1:
time: 23.1 us; the launch traced here: 22.9 us
  Pallas kernels  21.6 us (94%)
  local copies, waits for them, and re-layouts  0.66 us (3%)
  between operations  0.66 us (3%)
    pallas_call x1, Pallas kernels, on_device(): pl.pallas_call(functools.partial(kernel, dims), out_shape=pltpu.VMEM((1,...  21.6 us
    unnamed x1, local copies, waits for them, and re-layouts  0.66 us

profile of v1, /device:TPU:0, one launch (start us, length us, event | category | flops | bytes accessed | tf_op | source)
XLA Modules:
  0.0 22.9 jit_solution(6762429695626462261)
XLA Ops:
  0.7 21.6 %shard_map.109 = bf16[1,64,1024]{2,1,0:T(8,128)(2,1)S(1)} custom-call(s32[1,6]{1,0:T(1,128)} %ids_hbm.1, s32[1]{0:T(128)S(6)} %copy.14.counts_hbm, bf16[1,6,4,256]{3,2,1,0:T(4,128)(2,1)} %pixels_hbm.1, bf16[91,4,1024]{2,1,0:T(4,128)(2,1)} %table_hbm.1, bf16[91,1024]{1,0:T(8,128)(2,1)} %embed_hbm.1, f32[1,1024]{1,0:T(1,128)} %bitcast.2, f32[1,1024]{1,0:T(1,128)} %bitcast.3, ...), custom_call_target="tpu_custom_call" | custom-call | tf_op jit(solution)/shard_map/pallas_call | solution.py:371
  22.3 0.7 %copy.13 = bf16[1,64,1024]{2,1,0:T(8,128)(2,1)} copy(bf16[1,64,1024]{2,1,0:T(8,128)(2,1)S(1)} %shard_map.109) | data formatting | bytes 262144

commit v2 on v1

v2 whole, which is shorter than its diff:
```python
import functools
import math

import jax
import jax.numpy as jnp
from jax import lax
from jax.experimental import pallas as pl
from jax.experimental.pallas import tpu as pltpu
from jax.sharding import PartitionSpec as P

F32 = jnp.float32
BF16 = jnp.bfloat16
MESH = pl.DeviceIdType.MESH
PIECES = 3


def rounded_up(value, unit):
    return -(-value // unit) * unit


def flipped(index, bits):
    bit = 1
    while bit <= bits:
        if bits & bit:
            index = index + bit - 2 * bit * ((index // bit) % 2)
        bit *= 2
    return index


def pieces_of(value):
    parts = []
    for _ in range(PIECES):
        part = value.astype(BF16).astype(F32)
        parts.append(part)
        value = value - part
    return parts


def kernel(
    dims,
    pixels_hbm,
    ids_hbm,
    counts_hbm,
    table_hbm,
    embed_hbm,
    gain_hbm,
    bias_hbm,
    key_hbm,
    value_hbm,
    query_hbm,
    out_hbm,
    result_ref,
    ids_all,
    counts_ref,
    pix_all,
    table,
    embed,
    gain_ref,
    bias_ref,
    query_ref,
    key_block,
    value_all,
    wout,
    fold_all,
    own_rows,
    raw,
    left,
    field_ref,
    scale_all,
    scale_ref,
    weight_ref,
    mix_send,
    mix_recv,
    local_sem,
    send_sem,
    once_sem,
    value_rs,
    mix_rs,
):
    n, nv, groups, lo_size, slots, taps, patches, width, heads, head_size = dims
    hi_size = n // lo_size
    team = lo_size * nv
    mixers = lo_size * groups
    depth = key_block.shape[0]
    columns = key_block.shape[1]
    local_heads = heads // groups
    fold_rows = fold_all.shape[1]
    half = patches * groups // nv
    owned = patches // nv
    padded = own_rows.shape[1]
    every = nv * slots
    tap_rows = every * taps
    rows = raw.shape[1]
    tail = rows - tap_rows - every

    b = lax.axis_index("dp")
    v = lax.axis_index("var")
    hi, lo = b // lo_size, b % lo_size
    r, g = v // groups, v % groups
    me = lo * nv + v
    mixer = lo * groups + g

    def mate(bits):
        there = flipped(me, bits)
        return {"dp": hi * lo_size + there // nv, "var": there % nv}

    def remote(src, dst, ss, rs, where):
        return pltpu.make_async_remote_copy(
            src_ref=src, dst_ref=dst, send_sem=ss, recv_sem=rs, device_id=where, device_id_type=MESH
        )

    here = {"dp": b, "var": v}
    barrier = pltpu.get_barrier_semaphore()
    greeted = 0
    for off in range(1, n):
        pl.semaphore_signal(barrier, inc=1, device_id={"dp": (b + off) % n}, device_id_type=MESH)
        greeted += 1
    for bits in range(1, team):
        if bits % nv:
            pl.semaphore_signal(barrier, inc=1, device_id=mate(bits), device_id_type=MESH)
            greeted += 1

    mine = pl.ds(pl.multiple_of(g * columns, columns), columns)
    copies = [
        (query_hbm, query_ref),
        (key_hbm.at[:, mine], key_block),
        (value_hbm.at[:, mine], value_all.at[hi]),
        (ids_hbm, ids_all.at[me]),
        (pixels_hbm.at[0], pix_all.at[me]),
        (table_hbm, table),
        (embed_hbm, embed),
        (gain_hbm, gain_ref),
        (bias_hbm, bias_ref),
        (counts_hbm, counts_ref),
        (out_hbm, wout),
    ]
    gets = [pltpu.make_async_copy(s, d, local_sem.at[i]) for i, (s, d) in enumerate(copies)]
    for get in gets:
        get.start()
    (
        get_query,
        get_key,
        get_value,
        get_ids,
        get_pixels,
        get_table,
        get_embed,
        get_gain,
        get_bias,
        get_counts,
        get_out,
    ) = gets

    get_query.wait()
    own_query = query_ref[:local_heads]
    for i in range(1, groups):
        own_query = jnp.where(
            g == i, query_ref[i * local_heads : (i + 1) * local_heads], own_query
        )
    own_query = own_query * (1.0 / math.sqrt(head_size))
    if fold_rows > local_heads:
        blank = jnp.zeros((fold_rows - local_heads, head_size), F32)
        own_query = jnp.concatenate([own_query, blank], axis=0)
    own_head = (
        lax.broadcasted_iota(jnp.int32, (fold_rows, columns), 1) // head_size
        == lax.broadcasted_iota(jnp.int32, (fold_rows, columns), 0)
    )
    diagonal = jnp.where(own_head, jnp.concatenate([own_query] * local_heads, axis=1), 0.0)
    diagonal = jnp.concatenate(pieces_of(diagonal), axis=0).astype(BF16)
    get_key.wait()
    found = lax.dot_general(
        diagonal, key_block[...], (((1,), (1,)), ((), ())), preferred_element_type=F32
    )
    fold = found[:fold_rows]
    for i in range(1, PIECES):
        fold = fold + found[i * fold_rows : (i + 1) * fold_rows]
    fold_all[b] = fold

    get_value.wait()
    get_pixels.wait()
    get_ids.wait()
    pl.semaphore_wait(barrier, greeted)

    for bits in range(team - 1, 0, -1):
        remote(ids_all.at[me], ids_all.at[me], send_sem.at[0], once_sem.at[0], mate(bits)).start()
        remote(pix_all.at[me], pix_all.at[me], send_sem.at[1], once_sem.at[1], mate(bits)).start()
    for off in range(1, n):
        there = {"dp": (b + off) % n}
        remote(fold_all.at[b], fold_all.at[b], send_sem.at[3], once_sem.at[2], there).start()
    ring = sorted(range(1, hi_size), key=lambda off: -min(off, hi_size - off))
    for off in ring:
        there = {"dp": ((hi + off) % hi_size) * lo_size + lo}
        remote(value_all.at[hi], value_all.at[hi], send_sem.at[2], value_rs.at[off], there).start()

    get_table.wait()
    get_embed.wait()
    own_rows[...] = jnp.zeros_like(own_rows)
    ids_at = lax.broadcasted_iota(jnp.int32, (padded, embed.shape[0]), 0)
    wanted = jnp.full((padded, embed.shape[0]), -1, jnp.int32)
    for s in range(slots):
        chosen = ids_all[me, 0, s]
        found = table[chosen].astype(F32)
        for k in range(taps):
            own_rows[k, s : s + 1, :] = found[k : k + 1, :]
        wanted = jnp.where(ids_at == s, chosen, wanted)
    hot = (wanted == lax.broadcasted_iota(jnp.int32, wanted.shape, 1)).astype(BF16)
    own_rows[taps] = jnp.dot(hot, embed[...], preferred_element_type=F32)
    centred = []
    for k in range(taps + 1):
        row = own_rows[k]
        centred.append(row - jnp.mean(row, axis=-1, keepdims=True))
    pix = pix_all[me].astype(F32)
    fill = jnp.zeros((padded - slots, patches), F32)
    field = []
    for k in range(taps):
        own = [pix[s, k : k + 1, :] for s in range(slots)]
        field.append(jnp.concatenate(own + ([fill] if padded > slots else []), axis=0))
    field.append(jnp.ones((padded, patches), F32))
    variance = jnp.zeros((padded, patches), F32)
    for k in range(taps + 1):
        for m in range(k, taps + 1):
            gram = jnp.mean(centred[k] * centred[m], axis=-1, keepdims=True)
            variance += (1.0 if m == k else 2.0) * gram * (field[k] * field[m])
    scale = lax.rsqrt(jnp.maximum(variance, 0.0) + 1e-05)
    get_counts.wait()
    place = lax.broadcasted_iota(jnp.int32, (padded, patches), 0)
    live = (place < slots) & (v * slots + place < counts_ref[0])
    scale_all[me] = jnp.where(live, scale, -1.0)
    for bits in range(team - 1, 0, -1):
        remote(
            scale_all.at[me], scale_all.at[me], send_sem.at[4], once_sem.at[3], mate(bits)
        ).start()

    def arrived(ref, count, ss, rs):
        block = ref.at[pl.ds(0, count)]
        return remote(block, block, ss, rs, here)

    all_ids = arrived(ids_all, team - 1, send_sem.at[0], once_sem.at[0])
    all_ids.wait_recv()
    get_gain.wait()
    get_bias.wait()
    gain = gain_ref[...]
    slot_at = lax.broadcasted_iota(jnp.int32, (every, embed.shape[0]), 0)
    for j in range(lo_size):
        wanted = jnp.full((every, embed.shape[0]), -1, jnp.int32)
        for s in range(every):
            chosen = ids_all[j * nv + s // slots, 0, s % slots]
            raw[j, s * taps : (s + 1) * taps, :] = table[chosen].astype(F32)
            wanted = jnp.where(slot_at == s, chosen, wanted)
        hot = (wanted == lax.broadcasted_iota(jnp.int32, wanted.shape, 1)).astype(BF16)
        raw[j, tap_rows : tap_rows + every, :] = jnp.dot(
            hot, embed[...], preferred_element_type=F32
        )
        raw[j, tap_rows + every :, :] = jnp.zeros((tail, width), F32)
        row = raw[j, : tap_rows + every, :]
        row = (row - jnp.mean(row, axis=-1, keepdims=True)) * gain
        last = lax.broadcasted_iota(jnp.int32, (tail, width), 0)
        last = jnp.where(last == 0, bias_ref[...], 0.0)
        basis = jnp.concatenate([row, last], axis=0)
        for h in range(hi_size):
            at = h * lo_size * depth
            part = basis[:, at : at + depth]
            for other in range(1, lo_size):
                at += depth
                part = jnp.where(lo == other, basis[:, at : at + depth], part)
            left[h, j * rows : (j + 1) * rows, :] = part.astype(BF16)

    all_folds = arrived(fold_all, n - 1, send_sem.at[3], once_sem.at[2])
    all_folds.wait_recv()
    folded = jnp.concatenate([fold_all[i] for i in range(n)], axis=1)
    bias_score = jnp.sum(folded * bias_ref[...], axis=-1, keepdims=True)
    folded = folded * gain
    fold_sum = jnp.sum(folded, axis=-1, keepdims=True)
    keys = jnp.concatenate(pieces_of(folded) + [jnp.ones((8, width), F32)], axis=0).astype(BF16)

    all_pixels = arrived(pix_all, team - 1, send_sem.at[1], once_sem.at[1])
    all_pixels.wait_recv()
    all_scales = arrived(scale_all, team - 1, send_sem.at[4], once_sem.at[3])
    all_scales.wait_recv()
    window = pl.ds(pl.multiple_of(r * half, half), half)

    which = lax.broadcasted_iota(jnp.int32, (every, rows), 0)
    what = lax.broadcasted_iota(jnp.int32, (every, rows), 1)
    of_slot = jnp.where(what < tap_rows, what // taps, what - tap_rows) == which
    to_row = lax.broadcasted_iota(jnp.int32, (rows, every + 8), 0)
    of_row = jnp.where(to_row < tap_rows, to_row // taps, to_row - tap_rows)
    widen = (of_row == lax.broadcasted_iota(jnp.int32, (rows, every + 8), 1)).astype(BF16)

    for j in range(lo_size):
        for s in range(every):
            field_ref[s * taps : (s + 1) * taps, :] = pix_all[
                j * nv + s // slots, s % slots, :, window
            ].astype(F32)
        for i in range(nv):
            scale_ref[i * slots : (i + 1) * slots, :] = scale_all[j * nv + i, :slots, window]
        field_ref[tap_rows:, :] = jnp.ones((rows - tap_rows, half), F32)
        field = field_ref[...]
        scale = scale_ref[...]
        live = scale > 0.0

        found = lax.dot_general(
            keys, raw[j].astype(BF16), (((1,), (1,)), ((), ())), preferred_element_type=F32
        )
        score_of = found[:fold_rows]
        for i in range(1, PIECES):
            score_of = score_of + found[i * fold_rows : (i + 1) * fold_rows]
        row_sum = found[PIECES * fold_rows : PIECES * fold_rows + 1]
        score_of = score_of - (row_sum * (1.0 / width)) * fold_sum
        blocks = [
            jnp.where(of_slot, part[h : h + 1, :], 0.0)
            for h in range(local_heads)
            for part in pieces_of(score_of)
        ]
        slot_scores = jnp.dot(
            jnp.concatenate(blocks, axis=0).astype(BF16),
            field.astype(BF16),
            preferred_element_type=F32,
        )
        shares = []
        for h in range(local_heads):
            first = h * PIECES * every
            score = slot_scores[first : first + every]
            for i in range(1, PIECES):
                first += every
                score = score + slot_scores[first : first + every]
            score = score * scale + bias_score[h : h + 1, :]
            score = jnp.where(live, score, -1e30)
            expo = jnp.exp(score - jnp.max(score, axis=0, keepdims=True))
            prob = expo * (1.0 / jnp.sum(expo, axis=0, keepdims=True))
            whole = jnp.broadcast_to(jnp.sum(prob, axis=0, keepdims=True), (8, half))
            shares.append(jnp.concatenate([prob * scale, whole], axis=0))
        wide = jnp.dot(
            widen, jnp.concatenate(shares, axis=1).astype(BF16), preferred_element_type=F32
        )
        for h in range(local_heads):
            weight = wide[:, h * half : (h + 1) * half] * field
            weight_ref[j, :, h * rows : (h + 1) * rows] = weight.T.astype(BF16)

    projected = jnp.dot(left[hi], value_all[hi], preferred_element_type=F32)
    for off in ring[::-1]:
        src = (hi + hi_size - off) % hi_size
        remote(
            value_all.at[src], value_all.at[src], send_sem.at[2], value_rs.at[off], here
        ).wait_recv()
        projected += jnp.dot(left[src], value_all[src], preferred_element_type=F32)

    of_column = lax.broadcasted_iota(jnp.int32, (rows, columns), 1) // head_size
    for j in range(lo_size):
        part = projected[j * rows : (j + 1) * rows]
        spread = jnp.concatenate(
            [jnp.where(of_column == h, part, 0.0) for h in range(local_heads)], axis=0
        ).astype(BF16)
        mixed = jnp.dot(weight_ref[j], spread, preferred_element_type=F32).astype(BF16)
        mix_send[j * groups : (j + 1) * groups] = mixed.reshape(groups, owned, columns)

    for bits in range(mixers - 1, 0, -1):
        to = flipped(mixer, bits)
        there = {"dp": hi * lo_size + to // groups, "var": r * groups + to % groups}
        remote(
            mix_send.at[to], mix_recv.at[mixer], send_sem.at[5], mix_rs.at[bits], there
        ).start()

    get_out.wait()
    total = jnp.zeros((owned, width), F32)
    for near in range(groups):
        summed = None
        for far in range(lo_size):
            bits = far * groups + near
            src = flipped(mixer, bits)
            if bits:
                remote(
                    mix_send.at[src], mix_recv.at[src], send_sem.at[5], mix_rs.at[bits], here
                ).wait_recv()
                part = mix_recv[src].astype(F32)
            else:
                part = mix_send[src].astype(F32)
            summed = part if summed is None else summed + part
        there = pl.ds(pl.multiple_of(flipped(g, near) * columns, columns), columns)
        total += jnp.dot(summed.astype(BF16), wout[there, :], preferred_element_type=F32)
    result_ref[0] = total.astype(result_ref.dtype)

    all_ids.wait_send()
    all_pixels.wait_send()
    all_folds.wait_send()
    all_scales.wait_send()
    arrived(value_all, hi_size - 1, send_sem.at[2], value_rs.at[0]).wait_send()
    arrived(mix_send, mixers - 1, send_sem.at[5], mix_rs.at[0]).wait_send()


def on_device(
    n,
    nv,
    pixels,
    var_ids,
    counts,
    patch_weight,
    var_embed,
    norm_gain,
    norm_bias,
    key_weight,
    value_weight,
    query,
    out_weight,
):
    slots, taps, patches = pixels.shape[1:]
    width = out_weight.shape[0]
    heads, head_size = query.shape
    groups = min(nv, width // 128)
    lo_size = 2 if n % 2 == 0 else 1
    hi_size = n // lo_size
    team = lo_size * nv
    mixers = lo_size * groups
    columns = width // groups
    depth = value_weight.shape[0]
    padded = rounded_up(slots, 8)
    owned = patches // nv
    half = patches * groups // nv
    local_heads = heads // groups
    fold_rows = rounded_up(local_heads, 8)
    every = nv * slots
    rows = rounded_up(every * taps + every + 1, 16)
    hbm = pl.BlockSpec(memory_space=pltpu.HBM)
    vmem = pl.BlockSpec(memory_space=pltpu.VMEM)
    dims = (n, nv, groups, lo_size, slots, taps, patches, width, heads, head_size)
    dma = pltpu.SemaphoreType.DMA
    return pl.pallas_call(
        functools.partial(kernel, dims),
        out_shape=pltpu.VMEM((1, owned, width), BF16),
        in_specs=[hbm] * 11,
        out_specs=vmem,
        scratch_shapes=[
            pltpu.SMEM((team,) + var_ids.shape, jnp.int32),
            pltpu.SMEM(counts.shape, jnp.int32),
            pltpu.VMEM((team, slots, taps, patches), BF16),
            pltpu.VMEM(patch_weight.shape, BF16),
            pltpu.VMEM(var_embed.shape, BF16),
            pltpu.VMEM((1, width), F32),
            pltpu.VMEM((1, width), F32),
            pltpu.VMEM(query.shape, F32),
            pltpu.VMEM((depth, columns), BF16),
            pltpu.VMEM((hi_size, depth, columns), BF16),
            pltpu.VMEM((width, width), BF16),
            pltpu.VMEM((n, fold_rows, depth), F32),
            pltpu.VMEM((taps + 1, padded, width), F32),
            pltpu.VMEM((lo_size, rows, width), F32),
            pltpu.VMEM((hi_size, lo_size * rows, depth), BF16),
            pltpu.VMEM((rows, half), F32),
            pltpu.VMEM((team, padded, patches), F32),
            pltpu.VMEM((every, half), F32),
            pltpu.VMEM((lo_size, half, local_heads * rows), BF16),
            pltpu.VMEM((mixers, owned, columns), BF16),
            pltpu.VMEM((mixers, owned, columns), BF16),
            dma((11,)),
            dma((6,)),
            dma((4,)),
            dma((hi_size,)),
            dma((mixers,)),
        ],
        compiler_params=pltpu.CompilerParams(collective_id=0, has_side_effects=True),
    )(
        pixels,
        var_ids,
        counts,
        patch_weight,
        var_embed,
        norm_gain.reshape(1, width),
        norm_bias.reshape(1, width),
        key_weight,
        value_weight,
        query,
        out_weight,
    )


def solution(mesh):
    placed = (
        P("dp", "var", None, None),
        P("dp", "var"),
        P("dp"),
        P(),
        P(),
        P(),
        P(),
        P("dp", None),
        P("dp", None),
        P(),
        P(),
    )
    return jax.shard_map(
        functools.partial(on_device, mesh.shape["dp"], mesh.shape["var"]),
        mesh=mesh,
        in_specs=placed,
        out_specs=P("dp", "var", None),
        check_vma=False,
    )
```

time: 23.1 us -> 19.9 us (0.86)
  Pallas kernels: 21.6 us -> 18.4 us
    pallas_call x1, Pallas kernels: 21.6 us -> 18.4 us  [on_device(): pl.pallas_call(functools.partial(kernel, dims), out_shape=pltpu.VMEM((1,...]
where the time goes in v2:
time: 19.9 us; the launch traced here: 19.7 us
  Pallas kernels  18.4 us (92%)
  local copies, waits for them, and re-layouts  0.66 us (3%)
  between operations  0.66 us (3%)
    pallas_call x1, Pallas kernels, on_device(): pl.pallas_call(functools.partial(kernel, dims), out_shape=pltpu.VMEM((1,...  18.4 us
    unnamed x1, local copies, waits for them, and re-layouts  0.66 us

profile of v2, /device:TPU:0, one launch (start us, length us, event | category | flops | bytes accessed | tf_op | source)
XLA Modules:
  0.0 19.7 jit_solution(6651877899643034260)
XLA Ops:
  0.7 18.4 %shard_map.109 = bf16[1,64,1024]{2,1,0:T(8,128)(2,1)S(1)} custom-call(bf16[1,6,4,256]{3,2,1,0:T(4,128)(2,1)} %pixels_hbm.1, s32[1,6]{1,0:T(1,128)} %ids_hbm.1, s32[1]{0:T(128)S(6)} %copy.14.counts_hbm, bf16[91,4,1024]{2,1,0:T(4,128)(2,1)} %table_hbm.1, bf16[91,1024]{1,0:T(8,128)(2,1)} %embed_hbm.1, f32[1,1024]{1,0:T(1,128)} %bitcast.2, f32[1,1024]{1,0:T(1,128)} %bitcast.3, ...), custom_call_target="tpu_custom_call" | custom-call | tf_op jit(solution)/shard_map/pallas_call | solution.py:426
  19.0 0.7 %copy.13 = bf16[1,64,1024]{2,1,0:T(8,128)(2,1)} copy(bf16[1,64,1024]{2,1,0:T(8,128)(2,1)S(1)} %shard_map.109) | data formatting | bytes 262144

commit v3 on v2

--- a/solution.py
+++ b/solution.py
@@ -59,6 +59,7 @@
     bias_ref,
     query_ref,
     key_block,
+    value_send,
     value_all,
     wout,
     fold_all,
@@ -68,6 +69,7 @@
     field_ref,
     scale_all,
     scale_ref,
+    score_ref,
     weight_ref,
     mix_send,
     mix_recv,
@@ -83,6 +85,9 @@
     mixers = lo_size * groups
     depth = key_block.shape[0]
     columns = key_block.shape[1]
+    halves = value_all.shape[0]
+    strip = columns // halves
+    crossed = groups % 2 == 0
     local_heads = heads // groups
     fold_rows = fold_all.shape[1]
     half = patches * groups // nv
@@ -120,11 +125,22 @@
             pl.semaphore_signal(barrier, inc=1, device_id=mate(bits), device_id_type=MESH)
             greeted += 1
 
+    if crossed:
+        for off in range(1, hi_size):
+            there = {"dp": ((hi + off) % hi_size) * lo_size + lo, "var": flipped(v, 1)}
+            pl.semaphore_signal(barrier, inc=1, device_id=there, device_id_type=MESH)
+            greeted += 1
+    to_core = flipped(v, 1) if crossed else v
+    to_group = flipped(g, 1) if crossed else g
+
     mine = pl.ds(pl.multiple_of(g * columns, columns), columns)
+
+    def strip_of(group, a):
+        return pl.ds(pl.multiple_of(group * columns + a * strip, strip), strip)
+
     copies = [
         (query_hbm, query_ref),
         (key_hbm.at[:, mine], key_block),
-        (value_hbm.at[:, mine], value_all.at[hi]),
         (ids_hbm, ids_all.at[me]),
         (pixels_hbm.at[0], pix_all.at[me]),
         (table_hbm, table),
@@ -134,13 +150,17 @@
         (counts_hbm, counts_ref),
         (out_hbm, wout),
     ]
+    copies += [(value_hbm.at[:, strip_of(g, a)], value_all.at[a, hi]) for a in range(halves)]
+    copies[2:2] = [
+        (value_hbm.at[:, strip_of(to_group, a)], value_send.at[a]) for a in range(halves)
+    ]
     gets = [pltpu.make_async_copy(s, d, local_sem.at[i]) for i, (s, d) in enumerate(copies)]
     for get in gets:
         get.start()
+    get_query, get_key = gets[:2]
+    get_strips = gets[2 : 2 + halves]
+    get_values = gets[-halves:]
     (
-        get_query,
-        get_key,
-        get_value,
         get_ids,
         get_pixels,
         get_table,
@@ -149,7 +169,7 @@
         get_bias,
         get_counts,
         get_out,
-    ) = gets
+    ) = gets[2 + halves : -halves]
 
     get_query.wait()
     own_query = query_ref[:local_heads]
@@ -176,22 +196,8 @@
         fold = fold + found[i * fold_rows : (i + 1) * fold_rows]
     fold_all[b] = fold
 
-    get_value.wait()
+    get_ids.wait()
     get_pixels.wait()
-    get_ids.wait()
-    pl.semaphore_wait(barrier, greeted)
-
-    for bits in range(team - 1, 0, -1):
-        remote(ids_all.at[me], ids_all.at[me], send_sem.at[0], once_sem.at[0], mate(bits)).start()
-        remote(pix_all.at[me], pix_all.at[me], send_sem.at[1], once_sem.at[1], mate(bits)).start()
-    for off in range(1, n):
-        there = {"dp": (b + off) % n}
-        remote(fold_all.at[b], fold_all.at[b], send_sem.at[3], once_sem.at[2], there).start()
-    ring = sorted(range(1, hi_size), key=lambda off: -min(off, hi_size - off))
-    for off in ring:
-        there = {"dp": ((hi + off) % hi_size) * lo_size + lo}
-        remote(value_all.at[hi], value_all.at[hi], send_sem.at[2], value_rs.at[off], there).start()
-
     get_table.wait()
     get_embed.wait()
     own_rows[...] = jnp.zeros_like(own_rows)
@@ -226,10 +232,27 @@
     place = lax.broadcasted_iota(jnp.int32, (padded, patches), 0)
     live = (place < slots) & (v * slots + place < counts_ref[0])
     scale_all[me] = jnp.where(live, scale, -1.0)
+    for get in get_strips:
+        get.wait()
+    pl.semaphore_wait(barrier, greeted)
+
+    for bits in range(team - 1, 0, -1):
+        remote(ids_all.at[me], ids_all.at[me], send_sem.at[0], once_sem.at[0], mate(bits)).start()
+        remote(pix_all.at[me], pix_all.at[me], send_sem.at[1], once_sem.at[1], mate(bits)).start()
     for bits in range(team - 1, 0, -1):
         remote(
             scale_all.at[me], scale_all.at[me], send_sem.at[4], once_sem.at[3], mate(bits)
         ).start()
+    for off in range(1, n):
+        there = {"dp": (b + off) % n}
+        remote(fold_all.at[b], fold_all.at[b], send_sem.at[3], once_sem.at[2], there).start()
+    ring = sorted(range(1, hi_size), key=lambda off: -min(off, hi_size - off))
+    for a in range(halves):
+        for off in ring:
+            there = {"dp": ((hi + off) % hi_size) * lo_size + lo, "var": to_core}
+            remote(
+                value_send.at[a], value_all.at[a, hi], send_sem.at[2], value_rs.at[a, off], there
+            ).start()
 
     def arrived(ref, count, ss, rs):
         block = ref.at[pl.ds(0, count)]
@@ -273,12 +296,6 @@
     fold_sum = jnp.sum(folded, axis=-1, keepdims=True)
     keys = jnp.concatenate(pieces_of(folded) + [jnp.ones((8, width), F32)], axis=0).astype(BF16)
 
-    all_pixels = arrived(pix_all, team - 1, send_sem.at[1], once_sem.at[1])
-    all_pixels.wait_recv()
-    all_scales = arrived(scale_all, team - 1, send_sem.at[4], once_sem.at[3])
-    all_scales.wait_recv()
-    window = pl.ds(pl.multiple_of(r * half, half), half)
-
     which = lax.broadcasted_iota(jnp.int32, (every, rows), 0)
     what = lax.broadcasted_iota(jnp.int32, (every, rows), 1)
     of_slot = jnp.where(what < tap_rows, what // taps, what - tap_rows) == which
@@ -286,18 +303,8 @@
     of_row = jnp.where(to_row < tap_rows, to_row // taps, to_row - tap_rows)
     widen = (of_row == lax.broadcasted_iota(jnp.int32, (rows, every + 8), 1)).astype(BF16)
 
+    blocks = []
     for j in range(lo_size):
-        for s in range(every):
-            field_ref[s * taps : (s + 1) * taps, :] = pix_all[
-                j * nv + s // slots, s % slots, :, window
-            ].astype(F32)
-        for i in range(nv):
-            scale_ref[i * slots : (i + 1) * slots, :] = scale_all[j * nv + i, :slots, window]
-        field_ref[tap_rows:, :] = jnp.ones((rows - tap_rows, half), F32)
-        field = field_ref[...]
-        scale = scale_ref[...]
-        live = scale > 0.0
-
         found = lax.dot_general(
             keys, raw[j].astype(BF16), (((1,), (1,)), ((), ())), preferred_element_type=F32
         )
@@ -306,23 +313,39 @@
             score_of = score_of + found[i * fold_rows : (i + 1) * fold_rows]
         row_sum = found[PIECES * fold_rows : PIECES * fold_rows + 1]
         score_of = score_of - (row_sum * (1.0 / width)) * fold_sum
-        blocks = [
+        parts = [
             jnp.where(of_slot, part[h : h + 1, :], 0.0)
+            for part in pieces_of(score_of)
             for h in range(local_heads)
-            for part in pieces_of(score_of)
         ]
-        slot_scores = jnp.dot(
-            jnp.concatenate(blocks, axis=0).astype(BF16),
-            field.astype(BF16),
-            preferred_element_type=F32,
-        )
+        blocks.append(jnp.concatenate(parts, axis=0).astype(BF16))
+
+    all_pixels = arrived(pix_all, team - 1, send_sem.at[1], once_sem.at[1])
+    all_pixels.wait_recv()
+    window = pl.ds(pl.multiple_of(r * half, half), half)
+    for j in range(lo_size):
+        for s in range(every):
+            field_ref[j, s * taps : (s + 1) * taps, :] = pix_all[
+                j * nv + s // slots, s % slots, :, window
+            ].astype(F32)
+        field_ref[j, tap_rows:, :] = jnp.ones((rows - tap_rows, half), F32)
+        found = jnp.dot(blocks[j], field_ref[j].astype(BF16), preferred_element_type=F32)
+        every_head = local_heads * every
+        score = found[:every_head]
+        for i in range(1, PIECES):
+            score = score + found[i * every_head : (i + 1) * every_head]
+        score_ref[j] = score
+
+    all_scales = arrived(scale_all, team - 1, send_sem.at[4], once_sem.at[3])
+    all_scales.wait_recv()
+    for j in range(lo_size):
+        for i in range(nv):
+            scale_ref[j, i * slots : (i + 1) * slots, :] = scale_all[j * nv + i, :slots, window]
+        scale = scale_ref[j]
+        live = scale > 0.0
         shares = []
         for h in range(local_heads):
-            first = h * PIECES * every
-            score = slot_scores[first : first + every]
-            for i in range(1, PIECES):
-                first += every
-                score = score + slot_scores[first : first + every]
+            score = score_ref[j, h * every : (h + 1) * every, :]
             score = score * scale + bias_score[h : h + 1, :]
             score = jnp.where(live, score, -1e30)
             expo = jnp.exp(score - jnp.max(score, axis=0, keepdims=True))
@@ -333,58 +356,85 @@
             widen, jnp.concatenate(shares, axis=1).astype(BF16), preferred_element_type=F32
         )
         for h in range(local_heads):
-            weight = wide[:, h * half : (h + 1) * half] * field
+            weight = wide[:, h * half : (h + 1) * half] * field_ref[j]
             weight_ref[j, :, h * rows : (h + 1) * rows] = weight.T.astype(BF16)
 
-    projected = jnp.dot(left[hi], value_all[hi], preferred_element_type=F32)
-    for off in ring[::-1]:
-        src = (hi + hi_size - off) % hi_size
-        remote(
-            value_all.at[src], value_all.at[src], send_sem.at[2], value_rs.at[off], here
-        ).wait_recv()
-        projected += jnp.dot(left[src], value_all[src], preferred_element_type=F32)
-
-    of_column = lax.broadcasted_iota(jnp.int32, (rows, columns), 1) // head_size
-    for j in range(lo_size):
-        part = projected[j * rows : (j + 1) * rows]
-        spread = jnp.concatenate(
-            [jnp.where(of_column == h, part, 0.0) for h in range(local_heads)], axis=0
-        ).astype(BF16)
-        mixed = jnp.dot(weight_ref[j], spread, preferred_element_type=F32).astype(BF16)
-        mix_send[j * groups : (j + 1) * groups] = mixed.reshape(groups, owned, columns)
-
-    for bits in range(mixers - 1, 0, -1):
-        to = flipped(mixer, bits)
-        there = {"dp": hi * lo_size + to // groups, "var": r * groups + to % groups}
-        remote(
-            mix_send.at[to], mix_recv.at[mixer], send_sem.at[5], mix_rs.at[bits], there
-        ).start()
+    for get in get_values:
+        get.wait()
+    strip_heads = local_heads // halves
+    of_column = lax.broadcasted_iota(jnp.int32, (rows, strip), 1) // head_size
+    for a in range(halves):
+        projected = jnp.dot(left[hi], value_all[a, hi], preferred_element_type=F32)
+        for off in ring[::-1]:
+            src = (hi + hi_size - off) % hi_size
+            remote(
+                value_all.at[a, src],
+                value_all.at[a, src],
+                send_sem.at[2],
+                value_rs.at[a, off],
+                here,
+            ).wait_recv()
+            projected += jnp.dot(left[src], value_all[a, src], preferred_element_type=F32)
+        for far in range(lo_size - 1, -1, -1):
+            j = flipped(lo, far)
+            part = projected[:rows]
+            for other in range(1, lo_size):
+                part = jnp.where(j == other, projected[other * rows : (other + 1) * rows], part)
+            spread = jnp.concatenate(
+                [jnp.where(of_column == h, part, 0.0) for h in range(strip_heads)], axis=0
+            ).astype(BF16)
+            these = slice(a * strip_heads * rows, (a + 1) * strip_heads * rows)
+            mixed = jnp.dot(weight_ref[j, :, these], spread, preferred_element_type=F32)
+            mix_send[a, pl.ds(j * groups, groups)] = mixed.astype(BF16).reshape(
+                groups, owned, strip
+            )
+            for near in range(groups - 1, -1, -1):
+                bits = far * groups + near
+                if bits:
+                    to = flipped(mixer, bits)
+                    there = {"dp": hi * lo_size + to // groups, "var": r * groups + to % groups}
+                    remote(
+                        mix_send.at[a, to],
+                        mix_recv.at[a, mixer],
+                        send_sem.at[5],
+                        mix_rs.at[a, bits],
+                        there,
+                    ).start()
 
     get_out.wait()
     total = jnp.zeros((owned, width), F32)
-    for near in range(groups):
-        summed = None
-        for far in range(lo_size):
-            bits = far * groups + near
-            src = flipped(mixer, bits)
-            if bits:
-                remote(
-                    mix_send.at[src], mix_recv.at[src], send_sem.at[5], mix_rs.at[bits], here
-                ).wait_recv()
-                part = mix_recv[src].astype(F32)
-            else:
-                part = mix_send[src].astype(F32)
-            summed = part if summed is None else summed + part
-        there = pl.ds(pl.multiple_of(flipped(g, near) * columns, columns), columns)
-        total += jnp.dot(summed.astype(BF16), wout[there, :], preferred_element_type=F32)
+    for a in range(halves):
+        for near in range(groups):
+            summed = None
+            for far in range(lo_size):
+                bits = far * groups + near
+                src = flipped(mixer, bits)
+                if bits:
+                    remote(
+                        mix_send.at[a, src],
+                        mix_recv.at[a, src],
+                        send_sem.at[5],
+                        mix_rs.at[a, bits],
+                        here,
+                    ).wait_recv()
+                    part = mix_recv[a, src].astype(F32)
+                else:
+                    part = mix_send[a, src].astype(F32)
+                summed = part if summed is None else summed + part
+            total += jnp.dot(
+                summed.astype(BF16),
+                wout[strip_of(flipped(g, near), a), :],
+                preferred_element_type=F32,
+            )
     result_ref[0] = total.astype(result_ref.dtype)
 
     all_ids.wait_send()
     all_pixels.wait_send()
     all_folds.wait_send()
     all_scales.wait_send()
-    arrived(value_all, hi_size - 1, send_sem.at[2], value_rs.at[0]).wait_send()
-    arrived(mix_send, mixers - 1, send_sem.at[5], mix_rs.at[0]).wait_send()
+    for a in range(halves):
+        arrived(value_all.at[a], hi_size - 1, send_sem.at[2], value_rs.at[0, 0]).wait_send()
+        arrived(mix_send.at[a], mixers - 1, send_sem.at[5], mix_rs.at[0, 0]).wait_send()
 
 
 def on_device(
@@ -411,6 +461,8 @@
     team = lo_size * nv
     mixers = lo_size * groups
     columns = width // groups
+    halves = 2 if columns % 256 == 0 else 1
+    strip = columns // halves
     depth = value_weight.shape[0]
     padded = rounded_up(slots, 8)
     owned = patches // nv
@@ -438,23 +490,25 @@
             pltpu.VMEM((1, width), F32),
             pltpu.VMEM(query.shape, F32),
             pltpu.VMEM((depth, columns), BF16),
-            pltpu.VMEM((hi_size, depth, columns), BF16),
+            pltpu.VMEM((halves, depth, strip), BF16),
+            pltpu.VMEM((halves, hi_size, depth, strip), BF16),
             pltpu.VMEM((width, width), BF16),
             pltpu.VMEM((n, fold_rows, depth), F32),
             pltpu.VMEM((taps + 1, padded, width), F32),
             pltpu.VMEM((lo_size, rows, width), F32),
             pltpu.VMEM((hi_size, lo_size * rows, depth), BF16),
-            pltpu.VMEM((rows, half), F32),
+            pltpu.VMEM((lo_size, rows, half), F32),
             pltpu.VMEM((team, padded, patches), F32),
-            pltpu.VMEM((every, half), F32),
+            pltpu.VMEM((lo_size, every, half), F32),
+            pltpu.VMEM((lo_size, local_heads * every, half), F32),
             pltpu.VMEM((lo_size, half, local_heads * rows), BF16),
-            pltpu.VMEM((mixers, owned, columns), BF16),
-            pltpu.VMEM((mixers, owned, columns), BF16),
-            dma((11,)),
+            pltpu.VMEM((halves, mixers, owned, strip), BF16),
+            pltpu.VMEM((halves, mixers, owned, strip), BF16),
+            dma((10 + 2 * halves,)),
             dma((6,)),
             dma((4,)),
-            dma((hi_size,)),
-            dma((mixers,)),
+            dma((halves, hi_size)),
+            dma((halves, mixers)),
         ],
         compiler_params=pltpu.CompilerParams(collective_id=0, has_side_effects=True),
     )(

time: 19.9 us -> 19.2 us (0.965)
  Pallas kernels: 18.4 us -> 17.7 us
    pallas_call x1, Pallas kernels: 18.4 us -> 17.7 us  [on_device(): pl.pallas_call(functools.partial(kernel, dims), out_shape=pltpu.VMEM((1,...]
where the time goes in v3:
time: 19.2 us; the launch traced here: 19 us
  Pallas kernels  17.7 us (92%)
  local copies, waits for them, and re-layouts  0.66 us (3%)
  between operations  0.66 us (3%)
    pallas_call x1, Pallas kernels, on_device(): pl.pallas_call(functools.partial(kernel, dims), out_shape=pltpu.VMEM((1,...  17.7 us
    unnamed x1, local copies, waits for them, and re-layouts  0.66 us

profile of v3, /device:TPU:0, one launch (start us, length us, event | category | flops | bytes accessed | tf_op | source)
XLA Modules:
  0.0 19.0 jit_solution(12575296723865358132)
XLA Ops:
  0.7 17.7 %shard_map.109 = bf16[1,64,1024]{2,1,0:T(8,128)(2,1)S(1)} custom-call(bf16[1,6,4,256]{3,2,1,0:T(4,128)(2,1)} %pixels_hbm.1, s32[1,6]{1,0:T(1,128)} %ids_hbm.1, s32[1]{0:T(128)S(6)} %copy.14.counts_hbm, bf16[91,4,1024]{2,1,0:T(4,128)(2,1)} %table_hbm.1, bf16[91,1024]{1,0:T(8,128)(2,1)} %embed_hbm.1, f32[1,1024]{1,0:T(1,128)} %bitcast.2, f32[1,1024]{1,0:T(1,128)} %bitcast.3, ...), custom_call_target="tpu_custom_call" | custom-call | tf_op jit(solution)/shard_map/pallas_call | solution.py:478
  18.4 0.7 %copy.13 = bf16[1,64,1024]{2,1,0:T(8,128)(2,1)} copy(bf16[1,64,1024]{2,1,0:T(8,128)(2,1)S(1)} %shard_map.109) | data formatting | bytes 262144

commit v4 on v3

--- a/solution.py
+++ b/solution.py
@@ -18,13 +18,21 @@
     return -(-value // unit) * unit
 
 
-def flipped(index, bits):
-    bit = 1
-    while bit <= bits:
-        if bits & bit:
-            index = index + bit - 2 * bit * ((index // bit) % 2)
-        bit *= 2
-    return index
+class Bits:
+    def __init__(self, index, size):
+        self.index = index
+        self.steps = {}
+        bit = 1
+        while bit < size:
+            self.steps[bit] = bit - 2 * bit * lax.rem(lax.div(index, bit), 2)
+            bit *= 2
+
+    def flip(self, bits):
+        index = self.index
+        for bit, step in self.steps.items():
+            if bits & bit:
+                index = index + step
+        return index
 
 
 def pieces_of(value):
@@ -78,6 +86,7 @@
     once_sem,
     value_rs,
     mix_rs,
+    hand,
 ):
     n, nv, groups, lo_size, slots, taps, patches, width, heads, head_size = dims
     hi_size = n // lo_size
@@ -100,14 +109,28 @@
 
     b = lax.axis_index("dp")
     v = lax.axis_index("var")
-    hi, lo = b // lo_size, b % lo_size
-    r, g = v // groups, v % groups
+    hi, lo = lax.div(b, lo_size), lax.rem(b, lo_size)
+    r, g = lax.div(v, groups), lax.rem(v, groups)
     me = lo * nv + v
     mixer = lo * groups + g
+    my_lo, my_v = Bits(lo, lo_size), Bits(v, nv)
+    first_b = b - lo
 
     def mate(bits):
-        there = flipped(me, bits)
-        return {"dp": hi * lo_size + there // nv, "var": there % nv}
+        return {"dp": first_b + my_lo.flip(bits // nv), "var": my_v.flip(bits % nv)}
+
+    def partner_of(bits):
+        far, near = bits // groups, bits % groups
+        there = my_v.flip(near)
+        return my_lo.flip(far) * groups + there - r * groups, {
+            "dp": first_b + my_lo.flip(far),
+            "var": there,
+        }
+
+    def other_than(index, k):
+        return k + jnp.where(index <= k, 1, 0)
+
+    rings = [other_than(hi, k) for k in range(hi_size - 1)]
 
     def remote(src, dst, ss, rs, where):
         return pltpu.make_async_remote_copy(
@@ -115,23 +138,8 @@
         )
 
     here = {"dp": b, "var": v}
-    barrier = pltpu.get_barrier_semaphore()
-    greeted = 0
-    for off in range(1, n):
-        pl.semaphore_signal(barrier, inc=1, device_id={"dp": (b + off) % n}, device_id_type=MESH)
-        greeted += 1
-    for bits in range(1, team):
-        if bits % nv:
-            pl.semaphore_signal(barrier, inc=1, device_id=mate(bits), device_id_type=MESH)
-            greeted += 1
-
-    if crossed:
-        for off in range(1, hi_size):
-            there = {"dp": ((hi + off) % hi_size) * lo_size + lo, "var": flipped(v, 1)}
-            pl.semaphore_signal(barrier, inc=1, device_id=there, device_id_type=MESH)
-            greeted += 1
-    to_core = flipped(v, 1) if crossed else v
-    to_group = flipped(g, 1) if crossed else g
+    to_core = my_v.flip(1) if crossed else v
+    to_group = to_core - r * groups
 
     mine = pl.ds(pl.multiple_of(g * columns, columns), columns)
 
@@ -157,6 +165,37 @@
     gets = [pltpu.make_async_copy(s, d, local_sem.at[i]) for i, (s, d) in enumerate(copies)]
     for get in gets:
         get.start()
+
+    barrier = pltpu.get_barrier_semaphore()
+
+    def greet(where):
+        pl.semaphore_signal(barrier, inc=1, device_id=where, device_id_type=MESH)
+
+    core = lax.rem(v, 2)
+    partner = {"var": my_v.flip(1)}
+    if crossed:
+        for k, to in enumerate(rings):
+            ear = 1 if k == 0 else jnp.where(hi == 0, 1, 0)
+            for other in range(lo_size):
+                greet({"dp": to * lo_size + other, "var": v - core + ear})
+
+        @pl.when(core == 0)
+        def _():
+            greet(partner)
+            for bits in range(2, team, 2):
+                greet(mate(bits))
+
+        @pl.when(core == 1)
+        def _():
+            for bits in range(1, team, 2):
+                greet(mate(bits))
+    else:
+        for to in rings:
+            for other in range(lo_size):
+                greet({"dp": to * lo_size + other})
+        for bits in range(1, team):
+            greet(mate(bits))
+
     get_query, get_key = gets[:2]
     get_strips = gets[2 : 2 + halves]
     get_values = gets[-halves:]
@@ -196,8 +235,82 @@
         fold = fold + found[i * fold_rows : (i + 1) * fold_rows]
     fold_all[b] = fold
 
+    for get in get_strips:
+        get.wait()
     get_ids.wait()
     get_pixels.wait()
+
+    def send_fold(there):
+        remote(fold_all.at[b], fold_all.at[b], send_sem.at[3], once_sem.at[2], there).start()
+
+    def send_rows(some):
+        for to in some:
+            for other in range(lo_size):
+                send_fold({"dp": to * lo_size + other})
+        for a in range(halves):
+            for to in some:
+                there = {"dp": to * lo_size + lo, "var": to_core}
+                remote(
+                    value_send.at[a],
+                    value_all.at[a, hi],
+                    send_sem.at[2],
+                    value_rs.at[a, hi],
+                    there,
+                ).start()
+
+    def send_team():
+        for bits in range(1, team):
+            where = mate(bits)
+            remote(ids_all.at[me], ids_all.at[me], send_sem.at[0], once_sem.at[0], where).start()
+            remote(pix_all.at[me], pix_all.at[me], send_sem.at[1], once_sem.at[1], where).start()
+        for far in range(1, lo_size):
+            send_fold({"dp": first_b + my_lo.flip(far)})
+
+    def tell_partner():
+        pl.semaphore_signal(hand, inc=1, device_id=partner, device_id_type=MESH)
+
+    if crossed:
+        early, even = hi == 0, core == 0
+
+        @pl.when(early & even)
+        def _():
+            pl.semaphore_wait(barrier, team - 1)
+            tell_partner()
+            send_team()
+            pl.semaphore_wait(hand, 1)
+            send_rows(rings)
+
+        @pl.when(early & ~even)
+        def _():
+            pl.semaphore_wait(hand, 1)
+            send_team()
+            pl.semaphore_wait(barrier, 2 * (n - lo_size) + 1)
+            tell_partner()
+            send_rows(rings)
+
+        @pl.when(~early & even)
+        def _():
+            pl.semaphore_wait(hand, 1)
+            send_rows(rings[:1])
+            pl.semaphore_wait(barrier, team - 1 + 2 * (n - 2 * lo_size))
+            tell_partner()
+            send_rows(rings[1:])
+            send_team()
+
+        @pl.when(~early & ~even)
+        def _():
+            pl.semaphore_wait(barrier, 2 * lo_size + 1)
+            tell_partner()
+            send_rows(rings[:1])
+            pl.semaphore_wait(hand, 1)
+            send_rows(rings[1:])
+            send_team()
+
+    else:
+        pl.semaphore_wait(barrier, n - lo_size + team - 1)
+        send_rows(rings)
+        send_team()
+
     get_table.wait()
     get_embed.wait()
     own_rows[...] = jnp.zeros_like(own_rows)
@@ -232,27 +345,10 @@
     place = lax.broadcasted_iota(jnp.int32, (padded, patches), 0)
     live = (place < slots) & (v * slots + place < counts_ref[0])
     scale_all[me] = jnp.where(live, scale, -1.0)
-    for get in get_strips:
-        get.wait()
-    pl.semaphore_wait(barrier, greeted)
-
-    for bits in range(team - 1, 0, -1):
-        remote(ids_all.at[me], ids_all.at[me], send_sem.at[0], once_sem.at[0], mate(bits)).start()
-        remote(pix_all.at[me], pix_all.at[me], send_sem.at[1], once_sem.at[1], mate(bits)).start()
     for bits in range(team - 1, 0, -1):
         remote(
             scale_all.at[me], scale_all.at[me], send_sem.at[4], once_sem.at[3], mate(bits)
         ).start()
-    for off in range(1, n):
-        there = {"dp": (b + off) % n}
-        remote(fold_all.at[b], fold_all.at[b], send_sem.at[3], once_sem.at[2], there).start()
-    ring = sorted(range(1, hi_size), key=lambda off: -min(off, hi_size - off))
-    for a in range(halves):
-        for off in ring:
-            there = {"dp": ((hi + off) % hi_size) * lo_size + lo, "var": to_core}
-            remote(
-                value_send.at[a], value_all.at[a, hi], send_sem.at[2], value_rs.at[a, off], there
-            ).start()
 
     def arrived(ref, count, ss, rs):
         block = ref.at[pl.ds(0, count)]
@@ -365,41 +461,39 @@
     of_column = lax.broadcasted_iota(jnp.int32, (rows, strip), 1) // head_size
     for a in range(halves):
         projected = jnp.dot(left[hi], value_all[a, hi], preferred_element_type=F32)
-        for off in ring[::-1]:
-            src = (hi + hi_size - off) % hi_size
+        for src in rings:
             remote(
                 value_all.at[a, src],
                 value_all.at[a, src],
                 send_sem.at[2],
-                value_rs.at[a, off],
+                value_rs.at[a, src],
                 here,
             ).wait_recv()
             projected += jnp.dot(left[src], value_all[a, src], preferred_element_type=F32)
-        for far in range(lo_size - 1, -1, -1):
-            j = flipped(lo, far)
-            part = projected[:rows]
-            for other in range(1, lo_size):
-                part = jnp.where(j == other, projected[other * rows : (other + 1) * rows], part)
+        sent = 0
+        for j in range(lo_size):
+            part = projected[j * rows : (j + 1) * rows]
             spread = jnp.concatenate(
                 [jnp.where(of_column == h, part, 0.0) for h in range(strip_heads)], axis=0
             ).astype(BF16)
             these = slice(a * strip_heads * rows, (a + 1) * strip_heads * rows)
             mixed = jnp.dot(weight_ref[j, :, these], spread, preferred_element_type=F32)
-            mix_send[a, pl.ds(j * groups, groups)] = mixed.astype(BF16).reshape(
+            mix_send[a, j * groups : (j + 1) * groups] = mixed.astype(BF16).reshape(
                 groups, owned, strip
             )
-            for near in range(groups - 1, -1, -1):
-                bits = far * groups + near
-                if bits:
-                    to = flipped(mixer, bits)
-                    there = {"dp": hi * lo_size + to // groups, "var": r * groups + to % groups}
-                    remote(
-                        mix_send.at[a, to],
-                        mix_recv.at[a, mixer],
-                        send_sem.at[5],
-                        mix_rs.at[a, bits],
-                        there,
-                    ).start()
+            ready = (j + 1) * groups - 1
+            for k in range(sent, ready):
+                to = other_than(mixer, k)
+                to_lo = lax.div(to, groups)
+                there = {"dp": first_b + to_lo, "var": (r - to_lo) * groups + to}
+                remote(
+                    mix_send.at[a, to],
+                    mix_recv.at[a, mixer],
+                    send_sem.at[5],
+                    mix_rs.at[a, mixer],
+                    there,
+                ).start()
+            sent = ready
 
     get_out.wait()
     total = jnp.zeros((owned, width), F32)
@@ -408,13 +502,13 @@
             summed = None
             for far in range(lo_size):
                 bits = far * groups + near
-                src = flipped(mixer, bits)
+                src, _ = partner_of(bits)
                 if bits:
                     remote(
                         mix_send.at[a, src],
                         mix_recv.at[a, src],
                         send_sem.at[5],
-                        mix_rs.at[a, bits],
+                        mix_rs.at[a, src],
                         here,
                     ).wait_recv()
                     part = mix_recv[a, src].astype(F32)
@@ -423,7 +517,7 @@
                 summed = part if summed is None else summed + part
             total += jnp.dot(
                 summed.astype(BF16),
-                wout[strip_of(flipped(g, near), a), :],
+                wout[strip_of(my_v.flip(near) - r * groups, a), :],
                 preferred_element_type=F32,
             )
     result_ref[0] = total.astype(result_ref.dtype)
@@ -509,6 +603,7 @@
             dma((4,)),
             dma((halves, hi_size)),
             dma((halves, mixers)),
+            pltpu.SemaphoreType.REGULAR,
         ],
         compiler_params=pltpu.CompilerParams(collective_id=0, has_side_effects=True),
     )(

time: 19.2 us -> 18.2 us (0.948)
  the two profiles are of different devices: /device:TPU:0 before, /device:TPU:9 now
where the time goes in v4:
time: 18.2 us; the launch traced here: 18 us
  Pallas kernels  16.6 us (91%)
  local copies, waits for them, and re-layouts  0.66 us (4%)
  between operations  0.66 us (4%)
    pallas_call x1, Pallas kernels, on_device(): pl.pallas_call(functools.partial(kernel, dims), out_shape=pltpu.VMEM((1,...  16.6 us
    unnamed x1, local copies, waits for them, and re-layouts  0.66 us

profile of v4, /device:TPU:9, one launch (start us, length us, event | category | flops | bytes accessed | tf_op | source)
XLA Modules:
  0.0 18.0 jit_solution(17841011415285082347)
XLA Ops:
  0.7 16.6 %shard_map.109 = bf16[1,64,1024]{2,1,0:T(8,128)(2,1)S(1)} custom-call(bf16[1,6,4,256]{3,2,1,0:T(4,128)(2,1)} %pixels_hbm.1, s32[1,6]{1,0:T(1,128)} %ids_hbm.1, s32[1]{0:T(128)S(6)} %copy.14.counts_hbm, bf16[91,4,1024]{2,1,0:T(4,128)(2,1)} %table_hbm.1, bf16[91,1024]{1,0:T(8,128)(2,1)} %embed_hbm.1, f32[1,1024]{1,0:T(1,128)} %bitcast.2, f32[1,1024]{1,0:T(1,128)} %bitcast.3, ...), custom_call_target="tpu_custom_call" | custom-call | tf_op jit(solution)/shard_map/pallas_call | solution.py:572
  17.3 0.7 %copy.13 = bf16[1,64,1024]{2,1,0:T(8,128)(2,1)} copy(bf16[1,64,1024]{2,1,0:T(8,128)(2,1)S(1)} %shard_map.109) | data formatting | bytes 262144

commit v5 on v4

--- a/solution.py
+++ b/solution.py
@@ -376,13 +376,15 @@
         last = lax.broadcasted_iota(jnp.int32, (tail, width), 0)
         last = jnp.where(last == 0, bias_ref[...], 0.0)
         basis = jnp.concatenate([row, last], axis=0)
+        parts = []
         for h in range(hi_size):
             at = h * lo_size * depth
             part = basis[:, at : at + depth]
             for other in range(1, lo_size):
                 at += depth
                 part = jnp.where(lo == other, basis[:, at : at + depth], part)
-            left[h, j * rows : (j + 1) * rows, :] = part.astype(BF16)
+            parts.append(part)
+        left[j * rows : (j + 1) * rows, :] = jnp.concatenate(parts, axis=1).astype(BF16)
 
     all_folds = arrived(fold_all, n - 1, send_sem.at[3], once_sem.at[2])
     all_folds.wait_recv()
@@ -460,7 +462,6 @@
     strip_heads = local_heads // halves
     of_column = lax.broadcasted_iota(jnp.int32, (rows, strip), 1) // head_size
     for a in range(halves):
-        projected = jnp.dot(left[hi], value_all[a, hi], preferred_element_type=F32)
         for src in rings:
             remote(
                 value_all.at[a, src],
@@ -469,7 +470,11 @@
                 value_rs.at[a, src],
                 here,
             ).wait_recv()
-            projected += jnp.dot(left[src], value_all[a, src], preferred_element_type=F32)
+        projected = jnp.dot(
+            left[...],
+            value_all[a].reshape(hi_size * depth, strip),
+            preferred_element_type=F32,
+        )
         sent = 0
         for j in range(lo_size):
             part = projected[j * rows : (j + 1) * rows]
@@ -590,7 +595,7 @@
             pltpu.VMEM((n, fold_rows, depth), F32),
             pltpu.VMEM((taps + 1, padded, width), F32),
             pltpu.VMEM((lo_size, rows, width), F32),
-            pltpu.VMEM((hi_size, lo_size * rows, depth), BF16),
+            pltpu.VMEM((lo_size * rows, hi_size * depth), BF16),
             pltpu.VMEM((lo_size, rows, half), F32),
             pltpu.VMEM((team, padded, patches), F32),
             pltpu.VMEM((lo_size, every, half), F32),

time: 18.2 us -> 18.1 us (level)
  no operation moved by 1% of the time
where the time goes in v5:
time: 18.1 us; the launch traced here: 17.9 us
  Pallas kernels  16.5 us (91%)
  local copies, waits for them, and re-layouts  0.66 us (4%)
  between operations  0.66 us (4%)
    pallas_call x1, Pallas kernels, on_device(): pl.pallas_call(functools.partial(kernel, dims), out_shape=pltpu.VMEM((1,...  16.5 us
    unnamed x1, local copies, waits for them, and re-layouts  0.66 us

profile of v5, /device:TPU:9, one launch (start us, length us, event | category | flops | bytes accessed | tf_op | source)
XLA Modules:
  0.0 17.9 jit_solution(8996505640502242838)
XLA Ops:
  0.7 16.5 %shard_map.109 = bf16[1,64,1024]{2,1,0:T(8,128)(2,1)S(1)} custom-call(bf16[1,6,4,256]{3,2,1,0:T(4,128)(2,1)} %pixels_hbm.1, s32[1,6]{1,0:T(1,128)} %ids_hbm.1, s32[1]{0:T(128)S(6)} %copy.14.counts_hbm, bf16[91,4,1024]{2,1,0:T(4,128)(2,1)} %table_hbm.1, bf16[91,1024]{1,0:T(8,128)(2,1)} %embed_hbm.1, f32[1,1024]{1,0:T(1,128)} %bitcast.2, f32[1,1024]{1,0:T(1,128)} %bitcast.3, ...), custom_call_target="tpu_custom_call" | custom-call | tf_op jit(solution)/shard_map/pallas_call | solution.py:577
  17.2 0.7 %copy.13 = bf16[1,64,1024]{2,1,0:T(8,128)(2,1)} copy(bf16[1,64,1024]{2,1,0:T(8,128)(2,1)S(1)} %shard_map.109) | data formatting | bytes 262144

commit v6 on v5

--- a/solution.py
+++ b/solution.py
@@ -243,11 +243,13 @@
     def send_fold(there):
         remote(fold_all.at[b], fold_all.at[b], send_sem.at[3], once_sem.at[2], there).start()
 
-    def send_rows(some):
+    def send_folds(some):
         for to in some:
             for other in range(lo_size):
                 send_fold({"dp": to * lo_size + other})
-        for a in range(halves):
+
+    def send_values(some, strips):
+        for a in strips:
             for to in some:
                 there = {"dp": to * lo_size + lo, "var": to_core}
                 remote(
@@ -258,6 +260,19 @@
                     there,
                 ).start()
 
+    def send_rows(some):
+        send_folds(some)
+        send_values(some, range(halves))
+
+    def send_first():
+        send_folds(rings[:1])
+        send_values(rings[:1], range(1))
+
+    def send_rest():
+        send_folds(rings[1:])
+        send_values(rings[:1], range(1, halves))
+        send_values(rings[1:], range(halves))
+
     def send_team():
         for bits in range(1, team):
             where = mate(bits)
@@ -291,19 +306,19 @@
         @pl.when(~early & even)
         def _():
             pl.semaphore_wait(hand, 1)
-            send_rows(rings[:1])
+            send_first()
             pl.semaphore_wait(barrier, team - 1 + 2 * (n - 2 * lo_size))
             tell_partner()
-            send_rows(rings[1:])
+            send_rest()
             send_team()
 
         @pl.when(~early & ~even)
         def _():
             pl.semaphore_wait(barrier, 2 * lo_size + 1)
             tell_partner()
-            send_rows(rings[:1])
+            send_first()
             pl.semaphore_wait(hand, 1)
-            send_rows(rings[1:])
+            send_rest()
             send_team()
 
     else:
@@ -386,6 +401,16 @@
             parts.append(part)
         left[j * rows : (j + 1) * rows, :] = jnp.concatenate(parts, axis=1).astype(BF16)
 
+    all_pixels = arrived(pix_all, team - 1, send_sem.at[1], once_sem.at[1])
+    all_pixels.wait_recv()
+    window = pl.ds(pl.multiple_of(r * half, half), half)
+    for j in range(lo_size):
+        for s in range(every):
+            field_ref[j, s * taps : (s + 1) * taps, :] = pix_all[
+                j * nv + s // slots, s % slots, :, window
+            ].astype(F32)
+        field_ref[j, tap_rows:, :] = jnp.ones((rows - tap_rows, half), F32)
+
     all_folds = arrived(fold_all, n - 1, send_sem.at[3], once_sem.at[2])
     all_folds.wait_recv()
     folded = jnp.concatenate([fold_all[i] for i in range(n)], axis=1)
@@ -418,15 +443,7 @@
         ]
         blocks.append(jnp.concatenate(parts, axis=0).astype(BF16))
 
-    all_pixels = arrived(pix_all, team - 1, send_sem.at[1], once_sem.at[1])
-    all_pixels.wait_recv()
-    window = pl.ds(pl.multiple_of(r * half, half), half)
     for j in range(lo_size):
-        for s in range(every):
-            field_ref[j, s * taps : (s + 1) * taps, :] = pix_all[
-                j * nv + s // slots, s % slots, :, window
-            ].astype(F32)
-        field_ref[j, tap_rows:, :] = jnp.ones((rows - tap_rows, half), F32)
         found = jnp.dot(blocks[j], field_ref[j].astype(BF16), preferred_element_type=F32)
         every_head = local_heads * every
         score = found[:every_head]

time: 18.1 us -> 18 us (level)
  the two profiles are of different devices: /device:TPU:9 before, /device:TPU:25 now
where the time goes in v6:
time: 18 us; the launch traced here: 17.8 us
  Pallas kernels  16.4 us (91%)
  local copies, waits for them, and re-layouts  0.66 us (4%)
  between operations  0.66 us (4%)
    pallas_call x1, Pallas kernels, on_device(): pl.pallas_call(functools.partial(kernel, dims), out_shape=pltpu.VMEM((1,...  16.4 us
    unnamed x1, local copies, waits for them, and re-layouts  0.66 us

profile of v6, /device:TPU:25, one launch (start us, length us, event | category | flops | bytes accessed | tf_op | source)
XLA Modules:
  0.0 17.8 jit_solution(5182180809455905715)
XLA Ops:
  0.7 16.4 %shard_map.109 = bf16[1,64,1024]{2,1,0:T(8,128)(2,1)S(1)} custom-call(bf16[1,6,4,256]{3,2,1,0:T(4,128)(2,1)} %pixels_hbm.1, s32[1,6]{1,0:T(1,128)} %ids_hbm.1, s32[1]{0:T(128)S(6)} %copy.14.counts_hbm, bf16[91,4,1024]{2,1,0:T(4,128)(2,1)} %table_hbm.1, bf16[91,1024]{1,0:T(8,128)(2,1)} %embed_hbm.1, f32[1,1024]{1,0:T(1,128)} %bitcast.2, f32[1,1024]{1,0:T(1,128)} %bitcast.3, ...), custom_call_target="tpu_custom_call" | custom-call | tf_op jit(solution)/shard_map/pallas_call | solution.py:594
  17.1 0.7 %copy.13 = bf16[1,64,1024]{2,1,0:T(8,128)(2,1)} copy(bf16[1,64,1024]{2,1,0:T(8,128)(2,1)S(1)} %shard_map.109) | data formatting | bytes 262144
